TPU v7x, 512 devices: a whole 4x4x16 slice. The times are simulated.
512 devices in a mesh: chan: 128 (over y, z, core), grp: 4 (over x).
Axes of the slice: x: 4, y: 4, z: 16, core: 2. Of those that a mesh axis runs over, the one named last changes fastest.
Arguments:
- eta_pp: bfloat16 [512, 640, 640], P(('chan', 'grp'))
- ham_pp: bfloat16 [512, 640, 640], P(('chan', 'grp'))
- pp_factor: float32 [512, 640], P(('chan', 'grp')), may hold values from -1 to 1
- ph_factor: float32 [512, 640], P(('chan', 'grp')), may hold values from -1 to 1
- channel_size: int32 [512], P(('chan', 'grp')), may hold values from 320 to 640, as said below
- dest_dev: int32 [512, 160], P(('chan', 'grp')), may hold values from 0 to 127, as said below
- dest_sub: int32 [512, 160], P(('chan', 'grp')), may hold values from 0 to 159, as said below
- col_map: int32 [512, 640], P(('chan', 'grp')), may hold values from 0 to 639, each once within a row
- pair_swap: int32 [512, 640], P(('chan', 'grp')), may hold values from 0 to 639, as said below
Outputs:
- pp_flow: float32 [512, 640, 640], P(('chan', 'grp'))
- energy_flow: float32 [], replicated
Inputs may be any that keep to these rules, and one draw needn't show every extreme that they name: `channel_size`: a multiple of 4. `dest_dev`: every ph channel receives each of its 160 positions from exactly one pp subblock of its own group; from one pp channel at most 2 subblocks go to one ph channel, and exactly 2 for some. `dest_sub`: for each ph channel the positions it receives are all different. `pair_swap`: an involution of each channel's pairs without fixed points.
All inputs are finite; a program needn't handle non-finite values.
Results may differ from a plain program's by a relative error of at most 0.0036.
Values may be sent and summed in bfloat16 or wider, within the bound.
A program may use at most 64 MiB of HBM per device.

v0:
```python
import jax
import jax.numpy as jnp
from jax import lax
from jax.experimental import pallas as pl
from jax.experimental.pallas import tpu as pltpu
from jax.sharding import PartitionSpec as P

MESH = pl.DeviceIdType.MESH
HALF = jnp.bfloat16
FULL = jnp.float32
AXES = ("chan", "grp")

PEERS = 128
GROUPS = 4
Y, Z, CORES = 4, 16, 2
PLANE = GROUPS * Y * CORES
CAP = 640
SUBS = 160
STRIP = 4
SLOTS = 2
LINES = SLOTS * STRIP
ROWS = PEERS * LINES
STEP = 256
PART = 320


def dot(left, right):
    return jnp.dot(left, right, preferred_element_type=FULL)


def dot_t(left, right):
    return lax.dot_general(left, right, (((1,), (1,)), ((), ())), preferred_element_type=FULL)


def iota(shape, dim):
    return lax.broadcasted_iota(jnp.int32, shape, dim)


def one_hot(mask):
    return jnp.where(mask, 1.0, 0.0).astype(HALF)


def as_column(row):
    return jnp.transpose(jnp.broadcast_to(row, (128, row.shape[1])))


def at(i, size):
    return pl.ds(pl.multiple_of(i * size, size), size)


def kernel(
    size_ref, gen_ref, ham_ref, pp_ref, ph_ref, dev_ref, sub_ref, cols_ref, swap_ref,
    flow_ref, energy_ref,
    gm, hm, sent, note, got, got_note, left_g, left_h, sc_g, sc_h, mix_g, mix_h,
    ret, got_ret, ladder, column, column_dst, plane_sum, line_sum,
    send_sem, recv_sem, note_send, note_recv, ret_send, ret_recv,
    plane_send, plane_recv, line_send, line_recv,
):
    me = lax.axis_index("chan")
    grp = lax.axis_index("grp")
    my_y, my_z, my_c = me // 32, (me // 2) % 16, me % 2
    seat = grp * 8 + my_y * 2 + my_c

    barrier = pltpu.get_barrier_semaphore()

    def greet(k, carry):
        peer = lax.rem(me + k, PEERS)
        pl.semaphore_signal(barrier, inc=1, device_id={"chan": peer}, device_id_type=MESH)
        return carry

    def greet_plane(k, carry):
        other = lax.rem(grp + 1 + k // 8, GROUPS)
        peer = ((k // 2) % 4) * 32 + my_z * 2 + k % 2
        pl.semaphore_signal(
            barrier, inc=1, device_id={"chan": peer, "grp": other}, device_id_type=MESH
        )
        return carry

    lax.fori_loop(1, PEERS, greet, 0)
    lax.fori_loop(0, 24, greet_plane, 0)

    size = size_ref[0]
    inside = (iota((CAP, CAP), 0) < size) & (iota((CAP, CAP), 1) < size)
    gm[...] = jnp.where(inside, gen_ref[...].astype(FULL), 0.0).astype(HALF)
    hm[...] = jnp.where(inside, ham_ref[...].astype(FULL), 0.0).astype(HALF)

    target = dev_ref[...]
    hits = iota((PEERS, SUBS), 0) == target
    earlier = one_hot(iota((SUBS, SUBS), 0) < iota((SUBS, SUBS), 1))
    count = dot(one_hot(hits), earlier)
    rank = jnp.sum(jnp.where(hits, count, 0.0), axis=0, keepdims=True)
    place = sub_ref[...].astype(FULL) + 1.0
    first = jnp.sum(jnp.where(hits & (rank < 0.5), place, 0.0), axis=1, keepdims=True)
    second = jnp.sum(jnp.where(hits & (rank > 0.5), place, 0.0), axis=1, keepdims=True)
    lane = iota((PEERS, 128), 1)
    notes = jnp.where(lane == 0, first, jnp.where(lane == 1, second, 0.0))
    note[...] = notes.reshape(PEERS, 1, 128)

    slot = (2.0 * target.astype(FULL) + rank).astype(HALF)
    spread = one_hot(iota((SUBS, CAP), 1) // STRIP == iota((SUBS, CAP), 0))
    slots = dot(jnp.broadcast_to(slot, (16, SUBS)), spread)[0:1, :]
    dst = 4.0 * slots + (iota((1, CAP), 1) % STRIP).astype(FULL)
    dst_int = dst.astype(jnp.int32)
    column_dst[...] = as_column(dst).astype(jnp.int32)

    def pack(i, carry):
        pick = one_hot(iota((STEP, CAP), 0) + i * STEP == dst_int)
        g = dot(pick, gm[...]).reshape(STEP // LINES, LINES, CAP)
        h = dot(pick, hm[...]).reshape(STEP // LINES, LINES, CAP)
        sent[pl.ds(i * (STEP // LINES), STEP // LINES)] = jnp.concatenate([g, h], axis=1).astype(HALF)
        return carry

    lax.fori_loop(0, ROWS // STEP, pack, 0)

    pl.semaphore_wait(barrier, PEERS - 1 + 24)

    def send(k, carry):
        peer = lax.rem(me + k, PEERS)
        where = {"chan": peer}
        pltpu.make_async_remote_copy(
            note.at[peer], got_note.at[me], note_send, note_recv,
            device_id=where, device_id_type=MESH,
        ).start()
        pltpu.make_async_remote_copy(
            sent.at[peer], got.at[me], send_sem, recv_sem,
            device_id=where, device_id_type=MESH,
        ).start()
        return carry

    lax.fori_loop(1, PEERS, send, 0)
    got_note[pl.ds(me, 1)] = note[pl.ds(me, 1)]
    got[pl.ds(me, 1)] = sent[pl.ds(me, 1)]

    column[...] = as_column(pp_ref[...])
    sc_g[...] = (column[:, 0:1] * gm[...].astype(FULL)).astype(HALF)
    sc_h[...] = (column[:, 0:1] * hm[...].astype(FULL)).astype(HALF)

    def climb(i, trace):
        rows = at(i, PART)
        part = dot(gm[rows, :], sc_h[...]) - dot(hm[rows, :], sc_g[...])
        ladder[rows, :] = part
        on = iota((PART, CAP), 0) + i * PART == iota((PART, CAP), 1)
        return trace + jnp.sum(jnp.where(on, part, 0.0), axis=0, keepdims=True)

    trace = lax.fori_loop(0, CAP // PART, climb, jnp.zeros((1, CAP), FULL))
    trace = jnp.broadcast_to(jnp.sum(trace, axis=1, keepdims=True), (1, 128))
    plane_sum[pl.ds(seat, 1)] = trace.reshape(1, 1, 128)
    column[...] = as_column(ph_ref[...])

    def share(k, carry):
        @pl.when(k != seat)
        def _():
            pltpu.make_async_remote_copy(
                plane_sum.at[seat], plane_sum.at[seat], plane_send, plane_recv,
                device_id={"chan": ((k // 2) % 4) * 32 + my_z * 2 + k % 2, "grp": k // 8},
                device_id_type=MESH,
            ).start()
        return carry

    lax.fori_loop(0, PLANE, share, 0)

    def drain(ref, count, sem):
        pltpu.make_async_copy(ref.at[pl.ds(0, count)], ref.at[pl.ds(0, count)], sem).wait()

    drain(got_note, PEERS - 1, note_recv)
    flat = got_note[...].reshape(PEERS, 128).astype(HALF)
    r_slot = iota((PEERS, ROWS), 1) // STRIP
    placed = jnp.zeros((16, ROWS), FULL)
    for t in range(SLOTS):
        pick = one_hot(iota((16, 128), 1) == t)
        by_peer = dot_t(pick, flat).astype(HALF)
        placed += dot(by_peer, one_hot(r_slot == SLOTS * iota((PEERS, ROWS), 0) + t))
    source = 4 * (placed[0:1, :].astype(jnp.int32) - 1) + iota((1, ROWS), 1) % STRIP

    drain(got, PEERS - 1, recv_sem)

    def unpack(i, carry):
        block = got[pl.ds(i * (STEP // LINES), STEP // LINES)].astype(FULL)
        rows = at(i, STEP)
        left_g[rows, :] = block[:, 0:LINES, :].reshape(STEP, CAP).astype(HALF)
        left_h[rows, :] = block[:, LINES:, :].reshape(STEP, CAP).astype(HALF)
        return carry

    lax.fori_loop(0, ROWS // STEP, unpack, 0)

    def arrange(i, carry):
        rows = at(i, PART)
        pick = one_hot(iota((PART, ROWS), 0) + i * PART == source)
        scale = column[rows, 0:1]
        sc_g[rows, :] = (scale * dot(pick, left_g[...])).astype(HALF)
        sc_h[rows, :] = (scale * dot(pick, left_h[...])).astype(HALF)
        return carry

    lax.fori_loop(0, CAP // PART, arrange, 0)

    def permute(i, carry):
        rows = at(i, PART)
        pick = one_hot(iota((PART, CAP), 0) + i * PART == cols_ref[...])
        mix_g[rows, :] = dot(pick, sc_g[...]).astype(HALF)
        mix_h[rows, :] = dot(pick, sc_h[...]).astype(HALF)
        return carry

    lax.fori_loop(0, CAP // PART, permute, 0)

    drain(plane_sum, PLANE - 1, plane_recv)
    drain(plane_sum, PLANE - 1, plane_send)
    line_sum[pl.ds(my_z, 1)] = jnp.sum(plane_sum[...], axis=0, keepdims=True)

    def finish(i, carry):
        quarter = lax.rem(i + my_y, Y)
        rows = at(quarter, STEP)
        part = dot(left_g[rows, :], mix_h[...]) - dot(left_h[rows, :], mix_g[...])
        ret[pl.ds(quarter * 32, 32)] = part.reshape(32, LINES, CAP).astype(HALF)
        return carry

    lax.fori_loop(0, ROWS // STEP, finish, 0)

    def along(k, carry):
        peer = my_y * 32 + lax.rem(my_z + k, Z) * 2 + my_c
        pltpu.make_async_remote_copy(
            line_sum.at[my_z], line_sum.at[my_z], line_send, line_recv,
            device_id={"chan": peer}, device_id_type=MESH,
        ).start()
        return carry

    lax.fori_loop(1, Z, along, 0)

    def send_back(k, carry):
        peer = lax.rem(me + k, PEERS)
        pltpu.make_async_remote_copy(
            ret.at[peer], got_ret.at[me], ret_send, ret_recv,
            device_id={"chan": peer}, device_id_type=MESH,
        ).start()
        return carry

    lax.fori_loop(1, PEERS, send_back, 0)
    got_ret[pl.ds(me, 1)] = ret[pl.ds(me, 1)]

    drain(line_sum, Z - 1, line_recv)
    energy_ref[...] = 0.25 * jnp.sum(line_sum[...], axis=0)
    drain(note, PEERS - 1, note_send)
    drain(sent, PEERS - 1, send_sem)
    drain(got_ret, PEERS - 1, ret_recv)

    def unpack_back(i, carry):
        block = got_ret[pl.ds(i * (STEP // LINES), STEP // LINES)].astype(FULL)
        left_g[at(i, STEP), :] = block.reshape(STEP, CAP).astype(HALF)
        return carry

    lax.fori_loop(0, ROWS // STEP, unpack_back, 0)

    def gather(i, carry):
        rows = at(i, PART)
        pick = one_hot(iota((PART, ROWS), 1) == column_dst[rows, 0:1])
        sc_g[rows, :] = dot(pick, left_g[...]).astype(HALF)
        return carry

    lax.fori_loop(0, CAP // PART, gather, 0)
    partner = swap_ref[...]
    mix_g[...] = one_hot(iota((CAP, CAP), 0) == partner)

    def close(i, carry):
        rows = at(i, PART)
        own = sc_g[rows, :]
        swapped = dot(mix_g[rows, :], sc_g[...])
        anti = own.astype(FULL) - swapped - dot(own, mix_g[...]) + dot(swapped.astype(HALF), mix_g[...])
        live = (iota((PART, CAP), 0) + i * PART < size) & (iota((PART, CAP), 1) < size)
        flow_ref[rows, :] = jnp.where(live, 0.5 * ladder[rows, :] + anti, 0.0)
        return carry

    lax.fori_loop(0, CAP // PART, close, 0)
    drain(ret, PEERS - 1, ret_send)
    drain(line_sum, Z - 1, line_send)


def on_device(eta, ham, pp, ph, size, dev, sub, cols, swap):
    vmem = pl.BlockSpec(memory_space=pltpu.VMEM)
    half = lambda *s: pltpu.VMEM(s, HALF)
    full = lambda *s: pltpu.VMEM(s, FULL)
    flow, energy = pl.pallas_call(
        kernel,
        out_shape=(
            jax.ShapeDtypeStruct((CAP, CAP), FULL),
            jax.ShapeDtypeStruct((1, 128), FULL),
        ),
        in_specs=[pl.BlockSpec(memory_space=pltpu.SMEM)] + [vmem] * 8,
        out_specs=(vmem, vmem),
        scratch_shapes=[
            half(CAP, CAP), half(CAP, CAP),
            half(PEERS, 2 * LINES, CAP), full(PEERS, 1, 128),
            half(PEERS, 2 * LINES, CAP), full(PEERS, 1, 128),
            half(ROWS, CAP), half(ROWS, CAP),
            half(CAP, CAP), half(CAP, CAP), half(CAP, CAP), half(CAP, CAP),
            half(PEERS, LINES, CAP), half(PEERS, LINES, CAP),
            full(CAP, CAP), full(CAP, 128), pltpu.VMEM((CAP, 128), jnp.int32),
            full(PLANE, 1, 128), full(Z, 1, 128),
        ] + [pltpu.SemaphoreType.DMA] * 10,
        compiler_params=pltpu.CompilerParams(
            collective_id=0, has_side_effects=True, vmem_limit_bytes=60 << 20
        ),
    )(size, eta[0], ham[0], pp, ph, dev, sub, cols, swap)
    return flow[None], energy[0, 0]


def solution(mesh):
    return jax.shard_map(
        on_device,
        mesh=mesh,
        in_specs=(
            P(AXES, None, None), P(AXES, None, None), P(AXES, None), P(AXES, None), P(AXES),
            P(AXES, None), P(AXES, None), P(AXES, None), P(AXES, None),
        ),
        out_specs=(P(AXES, None, None), P()),
        check_vma=False,
    )
```

profile of v0, /device:TPU:1, one launch (start us, length us, event | category | flops | bytes accessed | tf_op | source)
XLA Modules:
  0.0 217.6 jit_solution(9213964557033570034)
XLA Ops:
  1.3 212.5 %shard_map.104 = (f32[640,640]{1,0:T(8,128)}, f32[1,128]{1,0:T(1,128)}) custom-call(s32[1]{0:T(128)S(6)} %copy.13.size_ref, bf16[640,640]{1,0:T(8,128)(2,1)} %bitcast.6, bf16[640,640]{1,0:T(8,128)(2,1)} %bitcast.7, f32[1,640]{1,0:T(1,128)} %pp_ref.1, f32[1,640]{1,0:T(1,128)} %ph_ref.1, s32[1,160]{1,0:T(1,128)} %dev_ref.1, s32[1,160]{1,0:T(1,128)} %sub_ref.1, ...), custom_call_target="tpu_custom_call" | custom-call | tf_op jit(solution)/shard_map/pallas_call | solution.py:280
  213.8 0.0 copy-start
  213.8 2.7 %copy.14 = f32[1,640,640]{2,1,0:T(8,128)} copy(f32[1,640,640]{2,1,0:T(8,128)} %bitcast.5) | data formatting | bytes 3276800
  216.5 0.0 copy-done
Async XLA Ops:
  213.8 2.7 %copy-start = (f32[1,128]{1,0:T(1,128)S(1)}, f32[1,128]{1,0:T(1,128)}, u32[]{:S(2)}) copy-start(f32[1,128]{1,0:T(1,128)} %get-tuple-element.5) | copy-start | bytes 1540
where the time goes:
time: 218 us
  Pallas kernels  212 us (97%)
  local copies, waits for them, and re-layouts  2.7 us (1%)
  between operations  2.46 us (1%)
    pallas_call x1, Pallas kernels, on_device(): pl.pallas_call(kernel, out_shape=(jax.ShapeDtypeStruct((CAP, CAP), FULL),...  212 us

commit v1 on v0

v1 whole, which is shorter than its diff:
```python
import jax
import jax.numpy as jnp
from jax import lax
from jax.experimental import pallas as pl
from jax.experimental.pallas import tpu as pltpu
from jax.sharding import PartitionSpec as P

MESH = pl.DeviceIdType.MESH
HALF = jnp.bfloat16
FULL = jnp.float32
AXES = ("chan", "grp")

PEERS = 128
GROUPS = 4
Y, Z, CORES = 4, 16, 2
PLANE = GROUPS * Y * CORES
CAP = 640
SUBS = 160
STRIP = 4
SLOTS = 2
LINES = SLOTS * STRIP
ROWS = PEERS * LINES
STEP = 256
PART = 320


def dot(left, right):
    return jnp.dot(left, right, preferred_element_type=FULL)


def dot_t(left, right):
    return lax.dot_general(left, right, (((1,), (1,)), ((), ())), preferred_element_type=FULL)


def iota(shape, dim):
    return lax.broadcasted_iota(jnp.int32, shape, dim)


def one_hot(mask):
    return jnp.where(mask, 1.0, 0.0).astype(HALF)


def as_column(row):
    return jnp.transpose(jnp.broadcast_to(row, (128, row.shape[1])))


def at(i, size):
    return pl.ds(pl.multiple_of(i * size, size), size)


def kernel(
    size_ref, gen_hbm, ham_hbm, pp_ref, ph_ref, dev_ref, sub_ref, cols_ref, swap_ref,
    flow_ref, energy_ref,
    gm, hm, sent, note, got, line_note, got_note, left_g, left_h, sc_g, sc_h, mix_g, mix_h,
    forward, backward, acc, both, ret, got_ret, ladder, column, column_dst, plane_sum, line_sum,
    load_sem, send_sem, recv_sem, note_send, note_recv, pass_send, pass_recv, ret_send, ret_recv,
    plane_send, plane_recv, line_send, line_recv,
):
    me = lax.axis_index("chan")
    grp = lax.axis_index("grp")
    my_y, my_z, my_c = me // 32, (me // 2) % 16, me % 2
    spot = my_y * 2 + my_c
    seat = grp * 8 + spot

    loads = [
        pltpu.make_async_copy(gen_hbm, gm, load_sem.at[0]),
        pltpu.make_async_copy(ham_hbm, hm, load_sem.at[1]),
    ]
    for load in loads:
        load.start()
    barrier = pltpu.get_barrier_semaphore()

    def chan_of(y, z, c):
        return lax.rem(y, Y) * 32 + lax.rem(z, Z) * 2 + lax.rem(c, CORES)

    def far_first(k):
        return my_z + 8 + ((k + 1) // 2) * (1 - 2 * (k % 2)) + Z

    def greet(k, carry):
        peer = chan_of(my_y + (k // 2) % 4, far_first(k // 8), my_c + k % 2)

        @pl.when(peer != me)
        def _():
            pl.semaphore_signal(barrier, inc=1, device_id={"chan": peer}, device_id_type=MESH)
        return carry

    def greet_plane(k, carry):
        other = lax.rem(grp + 1 + k // 8, GROUPS)
        peer = chan_of((k // 2) % 4, my_z, k % 2)
        pl.semaphore_signal(
            barrier, inc=1, device_id={"chan": peer, "grp": other}, device_id_type=MESH
        )
        return carry

    lax.fori_loop(0, PEERS, greet, 0)
    lax.fori_loop(0, 24, greet_plane, 0)

    target = dev_ref[...]
    seat_of = (target // 32 * 2 + target % 2) * Z + (target // 2) % Z
    hits = iota((PEERS, SUBS), 0) == seat_of
    earlier = one_hot(iota((SUBS, SUBS), 0) < iota((SUBS, SUBS), 1))
    count = dot(one_hot(hits), earlier)
    rank = jnp.sum(jnp.where(hits, count, 0.0), axis=0, keepdims=True)
    place = sub_ref[...].astype(FULL) + 1.0
    ranks = [
        jnp.sum(jnp.where(hits & (rank < 0.5), place, 0.0), axis=1, keepdims=True),
        jnp.sum(jnp.where(hits & (rank > 0.5), place, 0.0), axis=1, keepdims=True),
    ]
    lane = iota((Z, 128), 1)
    notes = jnp.zeros((Z, 128), FULL)
    for i in range(Y * CORES):
        for t in range(SLOTS):
            notes += jnp.where(lane == SLOTS * i + t, ranks[t][i * Z:(i + 1) * Z, :], 0.0)
    note[...] = notes.reshape(Z, 1, 128)

    slot = (2.0 * target.astype(FULL) + rank).astype(HALF)
    spread = one_hot(iota((SUBS, CAP), 1) // STRIP == iota((SUBS, CAP), 0))
    slots = dot(jnp.broadcast_to(slot, (16, SUBS)), spread)[0:1, :]
    dst = 4.0 * slots + (iota((1, CAP), 1) % STRIP).astype(FULL)
    dst_int = dst.astype(jnp.int32)

    for load in loads:
        load.wait()
    size = size_ref[...]
    inside = (iota((CAP, CAP), 0) < size) & (iota((CAP, CAP), 1) < size)
    gm[...] = jnp.where(inside, gm[...].astype(FULL), 0.0).astype(HALF)
    hm[...] = jnp.where(inside, hm[...].astype(FULL), 0.0).astype(HALF)

    def pack(i, carry):
        pick = one_hot(iota((STEP, CAP), 0) + i * STEP == dst_int)
        g = dot(pick, gm[...]).reshape(STEP // LINES, LINES, CAP)
        h = dot(pick, hm[...]).reshape(STEP // LINES, LINES, CAP)
        sent[pl.ds(i * 32, 32)] = jnp.concatenate([g, h], axis=1).astype(HALF)
        return carry

    lax.fori_loop(0, Y, pack, 0)

    pl.semaphore_wait(barrier, PEERS - 1 + 24)

    def drain(ref, start, count, sem):
        pltpu.make_async_copy(ref.at[pl.ds(start, count)], ref.at[pl.ds(start, count)], sem).wait()

    def send_quarter(src, dst_ref, i, out_sem, in_sem):
        def send(k, carry):
            peer = chan_of(my_y + i, far_first(k // 2), my_c + k % 2)

            def go():
                pltpu.make_async_remote_copy(
                    src.at[peer], dst_ref.at[me], out_sem, in_sem.at[i],
                    device_id={"chan": peer}, device_id_type=MESH,
                ).start()

            if i:
                go()
            else:
                pl.when(peer != me)(go)
            return carry

        lax.fori_loop(0, 32, send, 0)

    def came_from(i):
        return lax.rem(my_y + Y - i, Y)

    def wait_quarter(ref, i, sem):
        if i:
            drain(ref, came_from(i) * 32, 32, sem.at[i])
        else:
            drain(ref, 0, 31, sem.at[i])

    def note_line(k, carry):
        z = lax.rem(my_z + k, Z)
        pltpu.make_async_remote_copy(
            note.at[z], line_note.at[my_z], note_send, note_recv,
            device_id={"chan": chan_of(my_y, z, my_c)}, device_id_type=MESH,
        ).start()
        return carry

    lax.fori_loop(1, Z, note_line, 0)
    line_note[pl.ds(my_z, 1)] = note[pl.ds(my_z, 1)]
    got[pl.ds(me, 1)] = sent[pl.ds(me, 1)]
    send_quarter(sent, got, 0, send_sem, recv_sem)
    drain(line_note, 0, Z - 1, note_recv)

    def note_plane(k, carry):
        other = lax.rem(spot + k, 8)
        pltpu.make_async_remote_copy(
            line_note, got_note.at[spot], pass_send, pass_recv,
            device_id={"chan": chan_of(other // 2, my_z, other % 2)}, device_id_type=MESH,
        ).start()
        return carry

    lax.fori_loop(1, 8, note_plane, 0)
    for i in range(1, Y):
        send_quarter(sent, got, i, send_sem, recv_sem)
    got_note[pl.ds(spot, 1)] = line_note[...].reshape(1, Z, 1, 128)

    column[...] = as_column(pp_ref[...])
    sc_g[...] = (column[:, 0:1] * gm[...].astype(FULL)).astype(HALF)
    sc_h[...] = (column[:, 0:1] * hm[...].astype(FULL)).astype(HALF)

    def climb(i, trace):
        rows = at(i, PART)
        part = dot(gm[rows, :], sc_h[...]) - dot(hm[rows, :], sc_g[...])
        ladder[rows, :] = part
        on = iota((PART, CAP), 0) + i * PART == iota((PART, CAP), 1)
        return trace + jnp.sum(jnp.where(on, part, 0.0), axis=0, keepdims=True)

    trace = lax.fori_loop(0, CAP // PART, climb, jnp.zeros((1, CAP), FULL))
    trace = jnp.broadcast_to(jnp.sum(trace, axis=1, keepdims=True), (1, 128))
    plane_sum[pl.ds(seat, 1)] = trace.reshape(1, 1, 128)

    def share(k, carry):
        @pl.when(k != seat)
        def _():
            pltpu.make_async_remote_copy(
                plane_sum.at[seat], plane_sum.at[seat], plane_send, plane_recv,
                device_id={"chan": chan_of((k // 2) % 4, my_z, k % 2), "grp": k // 8},
                device_id_type=MESH,
            ).start()
        return carry

    lax.fori_loop(0, PLANE, share, 0)

    moved = iota((CAP, CAP), 0) == cols_ref[...]
    mix_g[...] = one_hot(moved)
    scale = jnp.sum(jnp.where(moved, ph_ref[...], 0.0), axis=1, keepdims=True)
    column[...] = jnp.broadcast_to(scale, (CAP, 128))
    swapped = iota((CAP, CAP), 0) == swap_ref[...]
    mix_h[...] = one_hot(swapped)
    dst_swapped = jnp.sum(jnp.where(swapped, dst, 0.0), axis=1, keepdims=True)
    column_dst[0:CAP, :] = as_column(dst).astype(jnp.int32)
    column_dst[CAP:, :] = jnp.broadcast_to(dst_swapped, (CAP, 128)).astype(jnp.int32)
    for q in range(Y):
        backward[q] = one_hot(iota((2 * CAP, STEP), 1) + q * STEP == column_dst[:, 0:1])

    drain(got_note, 0, 7, pass_recv)
    flat = got_note[...].reshape(PEERS, 128).astype(HALF)
    r_peer = iota((PEERS, ROWS), 1) // LINES
    r_seat = (r_peer // 32 * 2 + r_peer % 2) * Z + (r_peer // 2) % Z
    r_slot = iota((PEERS, ROWS), 1) // STRIP % SLOTS
    placed = jnp.zeros((16, ROWS), FULL)
    for t in range(SLOTS):
        pick = one_hot(iota((16, 128), 1) == SLOTS * spot + t)
        by_peer = dot_t(pick, flat).astype(HALF)
        placed += dot(by_peer, one_hot((r_seat == iota((PEERS, ROWS), 0)) & (r_slot == t)))
    source = 4 * (placed[0:1, :].astype(jnp.int32) - 1) + iota((1, ROWS), 1) % STRIP
    for q in range(Y):
        pick = one_hot(iota((CAP, STEP), 0) == source[:, q * STEP:(q + 1) * STEP])
        forward[q] = dot(mix_g[...], pick).astype(HALF)

    for i in range(Y):
        wait_quarter(got, i, recv_sem)
        q = came_from(i)
        block = got[pl.ds(q * 32, 32)].astype(FULL)
        g = block[:, 0:LINES, :].reshape(STEP, CAP).astype(HALF)
        h = block[:, LINES:, :].reshape(STEP, CAP).astype(HALF)
        left_g[at(q, STEP), :] = g
        left_h[at(q, STEP), :] = h
        part_g, part_h = dot(forward[q], g), dot(forward[q], h)
        if i == 0:
            acc[0:CAP, :] = part_g
            acc[CAP:, :] = part_h
        elif i < Y - 1:
            acc[0:CAP, :] += part_g
            acc[CAP:, :] += part_h
        else:
            sc_g[...] = (column[:, 0:1] * (acc[0:CAP, :] + part_g)).astype(HALF)
            sc_h[...] = (column[:, 0:1] * (acc[CAP:, :] + part_h)).astype(HALF)

    for i in range(Y):
        quarter = lax.rem(my_y + i, Y)
        rows = at(quarter, STEP)
        part = dot(left_g[rows, :], sc_h[...]) - dot(left_h[rows, :], sc_g[...])
        ret[pl.ds(quarter * 32, 32)] = part.reshape(32, LINES, CAP).astype(HALF)
        send_quarter(ret, got_ret, i, ret_send, ret_recv)
    got_ret[pl.ds(me, 1)] = ret[pl.ds(me, 1)]

    drain(plane_sum, 0, PLANE - 1, plane_recv)
    drain(plane_sum, 0, PLANE - 1, plane_send)
    line_sum[pl.ds(my_z, 1)] = jnp.sum(plane_sum[...], axis=0, keepdims=True)

    def along(k, carry):
        pltpu.make_async_remote_copy(
            line_sum.at[my_z], line_sum.at[my_z], line_send, line_recv,
            device_id={"chan": chan_of(my_y, my_z + k, my_c)}, device_id_type=MESH,
        ).start()
        return carry

    lax.fori_loop(1, Z, along, 0)

    drain(note, 0, Z - 1, note_send)
    drain(got_note, 0, 7, pass_send)
    drain(sent, 0, PEERS - 1, send_sem)

    for i in range(Y):
        wait_quarter(got_ret, i, ret_recv)
        q = came_from(i)
        block = got_ret[pl.ds(q * 32, 32)].astype(FULL).reshape(STEP, CAP).astype(HALF)
        part = dot(backward[q], block)
        if i == 0:
            acc[...] = part
        elif i < Y - 1:
            acc[...] += part
        else:
            both[...] = (acc[...] + part).astype(HALF)

    def close(i, carry):
        rows = at(i, PART)
        own = both[rows, :]
        other = both[pl.ds(pl.multiple_of(CAP + i * PART, PART), PART), :]
        anti = own.astype(FULL) - other.astype(FULL) - dot(own, mix_h[...]) + dot(other, mix_h[...])
        live = (iota((PART, CAP), 0) + i * PART < size) & (iota((PART, CAP), 1) < size)
        flow_ref[rows, :] = jnp.where(live, 0.5 * ladder[rows, :] + anti, 0.0)
        return carry

    lax.fori_loop(0, CAP // PART, close, 0)
    drain(line_sum, 0, Z - 1, line_recv)
    energy_ref[...] = 0.25 * jnp.sum(line_sum[...], axis=0)
    drain(ret, 0, PEERS - 1, ret_send)
    drain(line_sum, 0, Z - 1, line_send)


def on_device(eta, ham, pp, ph, size, dev, sub, cols, swap):
    vmem = pl.BlockSpec(memory_space=pltpu.VMEM)
    hbm = pl.BlockSpec(memory_space=pl.ANY)
    dma = pltpu.SemaphoreType.DMA
    half = lambda *s: pltpu.VMEM(s, HALF)
    full = lambda *s: pltpu.VMEM(s, FULL)
    flow, energy = pl.pallas_call(
        kernel,
        out_shape=(
            jax.ShapeDtypeStruct((CAP, CAP), FULL),
            jax.ShapeDtypeStruct((1, 128), FULL),
        ),
        in_specs=[vmem, hbm, hbm] + [vmem] * 6,
        out_specs=(vmem, vmem),
        scratch_shapes=[
            half(CAP, CAP), half(CAP, CAP),
            half(PEERS, 2 * LINES, CAP), full(Z, 1, 128),
            half(PEERS, 2 * LINES, CAP), full(Z, 1, 128), full(Y * CORES, Z, 1, 128),
            half(ROWS, CAP), half(ROWS, CAP),
            half(CAP, CAP), half(CAP, CAP), half(CAP, CAP), half(CAP, CAP),
            half(Y, CAP, STEP), half(Y, 2 * CAP, STEP), full(2 * CAP, CAP), half(2 * CAP, CAP),
            half(PEERS, LINES, CAP), half(PEERS, LINES, CAP),
            full(CAP, CAP), full(CAP, 128), pltpu.VMEM((2 * CAP, 128), jnp.int32),
            full(PLANE, 1, 128), full(Z, 1, 128),
            dma((2,)), dma, dma((Y,)), dma, dma, dma, dma, dma, dma((Y,)), dma, dma, dma, dma,
        ],
        compiler_params=pltpu.CompilerParams(
            collective_id=0, has_side_effects=True, vmem_limit_bytes=60 << 20
        ),
    )(size.reshape(1, 1), eta[0], ham[0], pp, ph, dev, sub, cols, swap)
    return flow[None], energy[0, 0]


def solution(mesh):
    return jax.shard_map(
        on_device,
        mesh=mesh,
        in_specs=(
            P(AXES, None, None), P(AXES, None, None), P(AXES, None), P(AXES, None), P(AXES),
            P(AXES, None), P(AXES, None), P(AXES, None), P(AXES, None),
        ),
        out_specs=(P(AXES, None, None), P()),
        check_vma=False,
    )
```

time: 218 us -> 207 us (0.950)
  Pallas kernels: 212 us -> 201 us
    pallas_call x1, Pallas kernels: 212 us -> 201 us  [on_device(): pl.pallas_call(kernel, out_shape=(jax.ShapeDtypeStruct((CAP, CAP), FULL),...]
where the time goes in v1:
time: 207 us
  Pallas kernels  201 us (97%)
  local copies, waits for them, and re-layouts  2.7 us (1%)
  between operations  2.46 us (1%)
    pallas_call x1, Pallas kernels, on_device(): pl.pallas_call(kernel, out_shape=(jax.ShapeDtypeStruct((CAP, CAP), FULL),...  201 us

profile of v1, /device:TPU:1, one launch (start us, length us, event | category | flops | bytes accessed | tf_op | source)
XLA Modules:
  0.0 206.5 jit_solution(4300877291522099770)
XLA Ops:
  1.3 201.4 %shard_map.104 = (f32[640,640]{1,0:T(8,128)}, f32[1,128]{1,0:T(1,128)}) custom-call(s32[1,1]{1,0:T(1,128)} %bitcast.6.size_ref, bf16[640,640]{1,0:T(8,128)(2,1)} %bitcast.8, bf16[640,640]{1,0:T(8,128)(2,1)} %bitcast.9, f32[1,640]{1,0:T(1,128)} %pp_ref.1, f32[1,640]{1,0:T(1,128)} %ph_ref.1, s32[1,160]{1,0:T(1,128)} %dev_ref.1, s32[1,160]{1,0:T(1,128)} %sub_ref.1, ...), custom_call_target="tpu_custom_call" | custom-call | tf_op jit(solution)/shard_map/pallas_call | solution.py:329
  202.7 0.0 copy-start
  202.7 2.7 %copy.14 = f32[1,640,640]{2,1,0:T(8,128)} copy(f32[1,640,640]{2,1,0:T(8,128)} %bitcast.7) | data formatting | bytes 3276800
  205.4 0.0 copy-done
Async XLA Ops:
  202.7 2.7 %copy-start = (f32[1,128]{1,0:T(1,128)S(1)}, f32[1,128]{1,0:T(1,128)}, u32[]{:S(2)}) copy-start(f32[1,128]{1,0:T(1,128)} %get-tuple-element.5) | copy-start | bytes 1540

commit v2 on v1

--- a/solution.py
+++ b/solution.py
@@ -52,7 +52,7 @@
     size_ref, gen_hbm, ham_hbm, pp_ref, ph_ref, dev_ref, sub_ref, cols_ref, swap_ref,
     flow_ref, energy_ref,
     gm, hm, sent, note, got, line_note, got_note, left_g, left_h, sc_g, sc_h, mix_g, mix_h,
-    forward, backward, acc, both, ret, got_ret, ladder, column, column_dst, plane_sum, line_sum,
+    forward, backward, acc, ret, got_ret, column, source, plane_sum, line_sum,
     load_sem, send_sem, recv_sem, note_send, note_recv, pass_send, pass_recv, ret_send, ret_recv,
     plane_send, plane_recv, line_send, line_recv,
 ):
@@ -121,7 +121,7 @@
 
     for load in loads:
         load.wait()
-    size = size_ref[...]
+    size = size_ref[0]
     inside = (iota((CAP, CAP), 0) < size) & (iota((CAP, CAP), 1) < size)
     gm[...] = jnp.where(inside, gm[...].astype(FULL), 0.0).astype(HALF)
     hm[...] = jnp.where(inside, hm[...].astype(FULL), 0.0).astype(HALF)
@@ -144,16 +144,12 @@
         def send(k, carry):
             peer = chan_of(my_y + i, far_first(k // 2), my_c + k % 2)
 
-            def go():
+            @pl.when(peer != me)
+            def _():
                 pltpu.make_async_remote_copy(
                     src.at[peer], dst_ref.at[me], out_sem, in_sem.at[i],
                     device_id={"chan": peer}, device_id_type=MESH,
                 ).start()
-
-            if i:
-                go()
-            else:
-                pl.when(peer != me)(go)
             return carry
 
         lax.fori_loop(0, 32, send, 0)
@@ -162,10 +158,13 @@
         return lax.rem(my_y + Y - i, Y)
 
     def wait_quarter(ref, i, sem):
-        if i:
+        @pl.when(i == 0)
+        def _():
+            drain(ref, 0, 31, sem.at[i])
+
+        @pl.when(i > 0)
+        def _():
             drain(ref, came_from(i) * 32, 32, sem.at[i])
-        else:
-            drain(ref, 0, 31, sem.at[i])
 
     def note_line(k, carry):
         z = lax.rem(my_z + k, Z)
@@ -190,8 +189,12 @@
         return carry
 
     lax.fori_loop(1, 8, note_plane, 0)
-    for i in range(1, Y):
+
+    def send_rest(i, carry):
         send_quarter(sent, got, i, send_sem, recv_sem)
+        return carry
+
+    lax.fori_loop(1, Y, send_rest, 0)
     got_note[pl.ds(spot, 1)] = line_note[...].reshape(1, Z, 1, 128)
 
     column[...] = as_column(pp_ref[...])
@@ -201,7 +204,7 @@
     def climb(i, trace):
         rows = at(i, PART)
         part = dot(gm[rows, :], sc_h[...]) - dot(hm[rows, :], sc_g[...])
-        ladder[rows, :] = part
+        flow_ref[rows, :] = 0.5 * part
         on = iota((PART, CAP), 0) + i * PART == iota((PART, CAP), 1)
         return trace + jnp.sum(jnp.where(on, part, 0.0), axis=0, keepdims=True)
 
@@ -226,12 +229,21 @@
     scale = jnp.sum(jnp.where(moved, ph_ref[...], 0.0), axis=1, keepdims=True)
     column[...] = jnp.broadcast_to(scale, (CAP, 128))
     swapped = iota((CAP, CAP), 0) == swap_ref[...]
-    mix_h[...] = one_hot(swapped)
-    dst_swapped = jnp.sum(jnp.where(swapped, dst, 0.0), axis=1, keepdims=True)
-    column_dst[0:CAP, :] = as_column(dst).astype(jnp.int32)
-    column_dst[CAP:, :] = jnp.broadcast_to(dst_swapped, (CAP, 128)).astype(jnp.int32)
-    for q in range(Y):
-        backward[q] = one_hot(iota((2 * CAP, STEP), 1) + q * STEP == column_dst[:, 0:1])
+    mix_h[...] = one_hot(swapped & (iota((CAP, CAP), 1) < size))
+    row = iota((CAP, 1), 0)
+    dst_own = as_column(dst)[:, 0:1].astype(jnp.int32)
+    dst_pair = jnp.sum(jnp.where(swapped, dst, 0.0), axis=1, keepdims=True).astype(jnp.int32)
+    dst_own = jnp.where(row < size, dst_own, -1)
+    dst_pair = jnp.where(row < size, dst_pair, -1)
+
+    def route_back(q, carry):
+        spots = iota((CAP, STEP), 1) + q * STEP
+        own = jnp.where(spots == dst_own, 1.0, 0.0)
+        backward[q] = (own - jnp.where(spots == dst_pair, 1.0, 0.0)).astype(HALF)
+        return carry
+
+    lax.fori_loop(0, Y, route_back, 0)
+    acc[...] = jnp.zeros((2 * CAP, CAP), FULL)
 
     drain(got_note, 0, 7, pass_recv)
     flat = got_note[...].reshape(PEERS, 128).astype(HALF)
@@ -243,12 +255,16 @@
         pick = one_hot(iota((16, 128), 1) == SLOTS * spot + t)
         by_peer = dot_t(pick, flat).astype(HALF)
         placed += dot(by_peer, one_hot((r_seat == iota((PEERS, ROWS), 0)) & (r_slot == t)))
-    source = 4 * (placed[0:1, :].astype(jnp.int32) - 1) + iota((1, ROWS), 1) % STRIP
-    for q in range(Y):
-        pick = one_hot(iota((CAP, STEP), 0) == source[:, q * STEP:(q + 1) * STEP])
+    source[...] = 4 * (placed[0:1, :].astype(jnp.int32) - 1) + iota((1, ROWS), 1) % STRIP
+
+    def route(q, carry):
+        pick = one_hot(iota((CAP, STEP), 0) == source[:, at(q, STEP)])
         forward[q] = dot(mix_g[...], pick).astype(HALF)
-
-    for i in range(Y):
+        return carry
+
+    lax.fori_loop(0, Y, route, 0)
+
+    def arrive(i, carry):
         wait_quarter(got, i, recv_sem)
         q = came_from(i)
         block = got[pl.ds(q * 32, 32)].astype(FULL)
@@ -256,64 +272,53 @@
         h = block[:, LINES:, :].reshape(STEP, CAP).astype(HALF)
         left_g[at(q, STEP), :] = g
         left_h[at(q, STEP), :] = h
-        part_g, part_h = dot(forward[q], g), dot(forward[q], h)
-        if i == 0:
-            acc[0:CAP, :] = part_g
-            acc[CAP:, :] = part_h
-        elif i < Y - 1:
-            acc[0:CAP, :] += part_g
-            acc[CAP:, :] += part_h
-        else:
-            sc_g[...] = (column[:, 0:1] * (acc[0:CAP, :] + part_g)).astype(HALF)
-            sc_h[...] = (column[:, 0:1] * (acc[CAP:, :] + part_h)).astype(HALF)
-
-    for i in range(Y):
+        acc[0:CAP, :] += dot(forward[q], g)
+        acc[CAP:, :] += dot(forward[q], h)
+        return carry
+
+    lax.fori_loop(0, Y, arrive, 0)
+    sc_g[...] = (column[:, 0:1] * acc[0:CAP, :]).astype(HALF)
+    sc_h[...] = (column[:, 0:1] * acc[CAP:, :]).astype(HALF)
+
+    def along(k, carry):
+        pltpu.make_async_remote_copy(
+            line_sum.at[my_z], line_sum.at[my_z], line_send, line_recv,
+            device_id={"chan": chan_of(my_y, my_z + k, my_c)}, device_id_type=MESH,
+        ).start()
+        return carry
+
+    def finish(i, carry):
         quarter = lax.rem(my_y + i, Y)
         rows = at(quarter, STEP)
         part = dot(left_g[rows, :], sc_h[...]) - dot(left_h[rows, :], sc_g[...])
         ret[pl.ds(quarter * 32, 32)] = part.reshape(32, LINES, CAP).astype(HALF)
         send_quarter(ret, got_ret, i, ret_send, ret_recv)
+
+        @pl.when(i == 0)
+        def _():
+            drain(plane_sum, 0, PLANE - 1, plane_recv)
+            drain(plane_sum, 0, PLANE - 1, plane_send)
+            line_sum[pl.ds(my_z, 1)] = jnp.sum(plane_sum[...], axis=0, keepdims=True)
+            lax.fori_loop(1, Z, along, 0)
+        return carry
+
+    lax.fori_loop(0, Y, finish, 0)
     got_ret[pl.ds(me, 1)] = ret[pl.ds(me, 1)]
-
-    drain(plane_sum, 0, PLANE - 1, plane_recv)
-    drain(plane_sum, 0, PLANE - 1, plane_send)
-    line_sum[pl.ds(my_z, 1)] = jnp.sum(plane_sum[...], axis=0, keepdims=True)
-
-    def along(k, carry):
-        pltpu.make_async_remote_copy(
-            line_sum.at[my_z], line_sum.at[my_z], line_send, line_recv,
-            device_id={"chan": chan_of(my_y, my_z + k, my_c)}, device_id_type=MESH,
-        ).start()
-        return carry
-
-    lax.fori_loop(1, Z, along, 0)
 
     drain(note, 0, Z - 1, note_send)
     drain(got_note, 0, 7, pass_send)
     drain(sent, 0, PEERS - 1, send_sem)
 
-    for i in range(Y):
+    def fold(i, carry):
         wait_quarter(got_ret, i, ret_recv)
         q = came_from(i)
         block = got_ret[pl.ds(q * 32, 32)].astype(FULL).reshape(STEP, CAP).astype(HALF)
-        part = dot(backward[q], block)
-        if i == 0:
-            acc[...] = part
-        elif i < Y - 1:
-            acc[...] += part
-        else:
-            both[...] = (acc[...] + part).astype(HALF)
-
-    def close(i, carry):
-        rows = at(i, PART)
-        own = both[rows, :]
-        other = both[pl.ds(pl.multiple_of(CAP + i * PART, PART), PART), :]
-        anti = own.astype(FULL) - other.astype(FULL) - dot(own, mix_h[...]) + dot(other, mix_h[...])
-        live = (iota((PART, CAP), 0) + i * PART < size) & (iota((PART, CAP), 1) < size)
-        flow_ref[rows, :] = jnp.where(live, 0.5 * ladder[rows, :] + anti, 0.0)
-        return carry
-
-    lax.fori_loop(0, CAP // PART, close, 0)
+        swap = dot(block, mix_h[...]).astype(HALF)
+        kept = jnp.where(iota((STEP, CAP), 1) < size, block.astype(FULL), 0.0).astype(HALF)
+        flow_ref[...] += dot(backward[q], kept) - dot(backward[q], swap)
+        return carry
+
+    lax.fori_loop(0, Y, fold, 0)
     drain(line_sum, 0, Z - 1, line_recv)
     energy_ref[...] = 0.25 * jnp.sum(line_sum[...], axis=0)
     drain(ret, 0, PEERS - 1, ret_send)
@@ -332,7 +337,7 @@
             jax.ShapeDtypeStruct((CAP, CAP), FULL),
             jax.ShapeDtypeStruct((1, 128), FULL),
         ),
-        in_specs=[vmem, hbm, hbm] + [vmem] * 6,
+        in_specs=[pl.BlockSpec(memory_space=pltpu.SMEM), hbm, hbm] + [vmem] * 6,
         out_specs=(vmem, vmem),
         scratch_shapes=[
             half(CAP, CAP), half(CAP, CAP),
@@ -340,16 +345,16 @@
             half(PEERS, 2 * LINES, CAP), full(Z, 1, 128), full(Y * CORES, Z, 1, 128),
             half(ROWS, CAP), half(ROWS, CAP),
             half(CAP, CAP), half(CAP, CAP), half(CAP, CAP), half(CAP, CAP),
-            half(Y, CAP, STEP), half(Y, 2 * CAP, STEP), full(2 * CAP, CAP), half(2 * CAP, CAP),
+            half(Y, CAP, STEP), half(Y, CAP, STEP), full(2 * CAP, CAP),
             half(PEERS, LINES, CAP), half(PEERS, LINES, CAP),
-            full(CAP, CAP), full(CAP, 128), pltpu.VMEM((2 * CAP, 128), jnp.int32),
+            full(CAP, 128), pltpu.VMEM((1, ROWS), jnp.int32),
             full(PLANE, 1, 128), full(Z, 1, 128),
             dma((2,)), dma, dma((Y,)), dma, dma, dma, dma, dma, dma((Y,)), dma, dma, dma, dma,
         ],
         compiler_params=pltpu.CompilerParams(
             collective_id=0, has_side_effects=True, vmem_limit_bytes=60 << 20
         ),
-    )(size.reshape(1, 1), eta[0], ham[0], pp, ph, dev, sub, cols, swap)
+    )(size, eta[0], ham[0], pp, ph, dev, sub, cols, swap)
     return flow[None], energy[0, 0]
 
 

time: 207 us -> 206 us (level)
  no operation moved by 1% of the time
where the time goes in v2:
time: 206 us
  Pallas kernels  200 us (97%)
  local copies, waits for them, and re-layouts  2.7 us (1%)
  between operations  2.46 us (1%)
    pallas_call x1, Pallas kernels, on_device(): pl.pallas_call(kernel, out_shape=(jax.ShapeDtypeStruct((CAP, CAP), FULL),...  200 us

profile of v2, /device:TPU:1, one launch (start us, length us, event | category | flops | bytes accessed | tf_op | source)
XLA Modules:
  0.0 205.5 jit_solution(16513802366262632812)
XLA Ops:
  1.3 200.4 %shard_map.104 = (f32[640,640]{1,0:T(8,128)}, f32[1,128]{1,0:T(1,128)}) custom-call(s32[1]{0:T(128)S(6)} %copy.13.size_ref, bf16[640,640]{1,0:T(8,128)(2,1)} %bitcast.6, bf16[640,640]{1,0:T(8,128)(2,1)} %bitcast.7, f32[1,640]{1,0:T(1,128)} %pp_ref.1, f32[1,640]{1,0:T(1,128)} %ph_ref.1, s32[1,160]{1,0:T(1,128)} %dev_ref.1, s32[1,160]{1,0:T(1,128)} %sub_ref.1, ...), custom_call_target="tpu_custom_call" | custom-call | tf_op jit(solution)/shard_map/pallas_call | solution.py:334
  201.6 0.0 copy-start
  201.7 2.7 %copy.14 = f32[1,640,640]{2,1,0:T(8,128)} copy(f32[1,640,640]{2,1,0:T(8,128)} %bitcast.5) | data formatting | bytes 3276800
  204.4 0.0 copy-done
Async XLA Ops:
  201.6 2.7 %copy-start = (f32[1,128]{1,0:T(1,128)S(1)}, f32[1,128]{1,0:T(1,128)}, u32[]{:S(2)}) copy-start(f32[1,128]{1,0:T(1,128)} %get-tuple-element.5) | copy-start | bytes 1540
